TPU v7x, 32 devices: a whole 2x2x4 slice. The times are simulated.
32 devices in a mesh: section: 2 (over x), expert: 16 (over z, y, core).
Axes of the slice: x: 2, y: 2, z: 4, core: 2. Of those that a mesh axis runs over, the one named last changes fastest.
Arguments:
- hidden_in: bfloat16 [2, 128, 3584], P(None, 'expert'), may hold values from -6 to 6
- layer_gain: float32 [2, 3584], P('section'), may hold values from 0.25 to 1.75
- router: bfloat16 [2, 3584, 4], P('section'), may hold values from -0.09375 to 0.09375
- w_gate: bfloat16 [2, 3584, 8192], P('section', None, 'expert'), may hold values from -0.09375 to 0.09375
- w_up: bfloat16 [2, 3584, 8192], P('section', None, 'expert'), may hold values from -0.09375 to 0.09375
- w_down: bfloat16 [2, 8192, 3584], P('section', 'expert'), may hold values from -0.125 to 0.125
- final_gain: float32 [3584], replicated, may hold values from 0.25 to 1.75
- head: bfloat16 [8192, 3584], P(('section', 'expert')), may hold values from -18.775102 to 18.775102
- routing: int32 [2, 2, 128, 2], P('section', None, 'expert'), may hold values from 0 to 3, all different within a row; in each aligned block of 8 rows (0 to 7, 8 to 15, ..., all dimensions but the last counted through in order) at most 4 rows name the same one
- targets: int32 [2, 128], replicated, may hold values from 0 to 8191
- seq_ids: int32 [2, 128], replicated, may hold values from 0 to 3, never falling along the last dimension, each value on 1 to 64 neighbouring positions
Outputs:
- token_logprob: float32 [2, 128], P(None, 'expert')
- seq_mean: float32 [2, 4], replicated
Inputs may be any that keep to these rules, and one draw needn't show every extreme that they name: `routing`: in each aligned block of 8 tokens (the tokens of one device) a token's 2 experts differ and no expert is named by more than 4 tokens; some expert is named by exactly 4. `seq_ids`: ids never fall along a micro-batch's tokens; each of the 4 ids occurs on 1 to 64 tokens, one on exactly 64.
All inputs are finite; a program needn't handle non-finite values.
Results may differ from a plain program's by a relative error of at most 0.014.
Values may be sent and summed in bfloat16 or wider, within the bound.
A program may use at most 64 MiB of HBM per device.

v0:
```python
import jax
import jax.numpy as jnp
from jax import lax
from jax.sharding import PartitionSpec as P

SEQS = 4


def shifted(shard, axis, by):
    size = lax.axis_size(axis)
    pairs = [(i, i + by) for i in range(size) if 0 <= i + by < size]
    return lax.ppermute(shard, axis, pairs)


def broadcast(block, axis, holder):
    block = jnp.where(lax.axis_index(axis) == holder, block, jnp.zeros_like(block))
    return lax.psum(block, axis)


def rms_scale(states, gain):
    values = states.astype(jnp.float32)
    factor = lax.rsqrt(jnp.mean(values * values, -1, keepdims=True) + 1e-06)
    return values * factor * gain


def body(
    hidden_in, layer_gain, router, w_gate, w_up, w_down, final_gain, head, routing, targets, seq_ids
):
    micro_count, tok_count, model_width = hidden_in.shape
    expert_count = router.shape[2]
    top_count = routing.shape[3]
    sections = lax.axis_size("section")
    members = lax.axis_size("expert")
    section_pos = lax.axis_index("section")
    member_pos = lax.axis_index("expert")
    split_count = members // expert_count
    capacity = min(tok_count, 9 * tok_count * top_count // (8 * expert_count))
    tick_count = micro_count + sections - 1

    def expert_rows(incoming):
        sources, slot_count, width_in = incoming.shape
        flat_rows = incoming.reshape(sources * slot_count, width_in)
        gate_val = jnp.dot(flat_rows, w_gate[0], preferred_element_type=jnp.float32)
        up_val = jnp.dot(flat_rows, w_up[0], preferred_element_type=jnp.float32)
        inner = (jax.nn.silu(gate_val) * up_val).astype(jnp.bfloat16)
        partial_value = jnp.dot(inner, w_down[0], preferred_element_type=jnp.float32).astype(
            jnp.bfloat16
        )
        return lax.all_to_all(
            partial_value.reshape(sources, slot_count, width_in),
            "expert",
            split_axis=0,
            concat_axis=0,
            tiled=True,
        )

    def expert_layer(states, micro_pos):
        route_ids = lax.dynamic_index_in_dim(routing[0], micro_pos, 0, keepdims=False)
        normed = rms_scale(states, layer_gain[0]).astype(jnp.bfloat16)
        logits = jnp.dot(normed, router[0], preferred_element_type=jnp.float32)
        chosen = route_ids[:, :, None] == jnp.arange(expert_count, dtype=jnp.int32)[None, None, :]
        affinity = jax.nn.sigmoid(jnp.sum(jnp.where(chosen, logits[:, None, :], 0.0), -1))
        weight = affinity / jnp.sum(affinity, -1, keepdims=True)
        flags = chosen.reshape(tok_count * top_count, expert_count).astype(jnp.int32)
        ranks = jnp.cumsum(flags, 0) - flags
        slot_ids = jnp.sum(ranks * flags, -1).reshape(tok_count, top_count)
        destination = route_ids * capacity + slot_ids
        places = jnp.arange(expert_count * capacity, dtype=jnp.int32)
        table = jnp.any(places[:, None, None] == destination[None], -1).astype(jnp.bfloat16)
        packed = jnp.dot(table, normed, preferred_element_type=jnp.float32).astype(jnp.bfloat16)
        outgoing = jnp.broadcast_to(
            packed.reshape(expert_count, 1, capacity, model_width),
            (expert_count, split_count, capacity, model_width),
        )
        outgoing = outgoing.reshape(members, capacity, model_width)
        returned = expert_rows(
            lax.all_to_all(outgoing, "expert", split_axis=0, concat_axis=0, tiled=True)
        )
        summed = jnp.sum(
            returned.reshape(expert_count, split_count, capacity, model_width).astype(jnp.float32),
            1,
        )
        summed = summed.reshape(expert_count * capacity, model_width)
        picked = summed[destination]
        mixed = jnp.sum(weight[:, :, None] * picked, 1)
        return (states.astype(jnp.float32) + 2.5 * mixed).astype(jnp.bfloat16)

    def advance(step, carry):
        arrived, record = carry
        entering = lax.dynamic_index_in_dim(
            hidden_in, jnp.minimum(step, micro_count - 1), 0, keepdims=False
        )
        states = jnp.where(section_pos == 0, entering, arrived)
        micro_pos = jnp.clip(step - section_pos, 0, micro_count - 1)
        result = expert_layer(states, micro_pos)
        finished = step - (sections - 1)
        record_pos = jnp.clip(finished, 0, micro_count - 1)
        keeping = (finished >= 0) & (section_pos == sections - 1)
        previous = lax.dynamic_index_in_dim(record, record_pos, 0, keepdims=False)
        record = lax.dynamic_update_index_in_dim(
            record, jnp.where(keeping, result, previous), record_pos, 0
        )
        arrived = shifted(result, "section", 1)
        return (arrived, record)

    start_rows = jnp.zeros((tok_count, model_width), jnp.bfloat16)
    start_record = jnp.zeros((micro_count, tok_count, model_width), jnp.bfloat16)
    arrived, record = lax.fori_loop(0, tick_count, advance, (start_rows, start_record))
    shared = broadcast(record, "section", sections - 1)
    normed = rms_scale(lax.all_gather(shared, "expert", axis=1, tiled=True), final_gain).astype(
        jnp.bfloat16
    )
    logits = jnp.einsum("mrd,vd->mrv", normed, head, preferred_element_type=jnp.float32)
    voc_count = head.shape[0]
    vocab_start = (section_pos * members + member_pos) * voc_count
    vocab_ids = vocab_start + jnp.arange(voc_count, dtype=jnp.int32)
    target_hit = targets[:, :, None] == vocab_ids[None, None, :]
    target_part = jnp.sum(jnp.where(target_hit, logits, 0.0), -1)
    local_max = jnp.max(logits, -1)
    peak = lax.pmax(local_max, ("section", "expert"))
    local_sum = jnp.sum(jnp.exp(logits - peak[..., None]), -1)
    total, target_logit = lax.psum((local_sum, target_part), ("section", "expert"))
    logprob = target_logit - (peak + jnp.log(total))
    token_part = lax.dynamic_slice_in_dim(logprob, member_pos * tok_count, tok_count, 1)
    member = seq_ids[:, :, None] == jnp.arange(SEQS, dtype=jnp.int32)[None, None, :]
    sums = jnp.sum(jnp.where(member, logprob[..., None], 0.0), 1)
    counts = jnp.sum(member.astype(jnp.float32), 1)
    return (token_part, sums / counts)


def solution(mesh):
    return jax.shard_map(
        body,
        mesh=mesh,
        in_specs=(
            P(None, "expert", None),
            P("section", None),
            P("section", None, None),
            P("section", None, "expert"),
            P("section", None, "expert"),
            P("section", "expert", None),
            P(),
            P(("section", "expert"), None),
            P("section", None, "expert", None),
            P(),
            P(),
        ),
        out_specs=(P(None, "expert"), P()),
        check_vma=False,
    )
```

profile of v0, /device:TPU:0, one launch (start us, length us, event | category | flops | bytes accessed | tf_op | source)
XLA Modules:
  0.0 332.3 jit_solution(14966221587501759313)
XLA Ops:
  7.3 167.9 %while.17 = (s32[]{:T(128)}, bf16[8,3584]{1,0:T(8,128)(2,1)S(1)}, bf16[2,8,3584]{2,1,0:T(8,128)(2,1)S(1)}, pred[]{:T(512)}, bf16[2,8,3584]{2,1,0:T(8,128)(2,1)},...) while((s32[]{:T(128)}, bf16[8,3584]{1,0:T(8,128)(2,1)S(1)}, ...), condition=%wide.region_9.10_spmd, body=%wide.region_0.9_spmd.sunk | while | flops 707251328 | bytes 21631636 | solution.py:108
  7.3 0.8 constant_dynamic-slice_fusion.6
  8.7 0.7 multiply_add_fusion.2
  9.5 1.0 fusion.70
  10.5 0.8 reduce.2
  11.5 0.9 broadcast_in_dim.134
  12.4 7.4 %all-to-all-start = ((bf16[16,4,3584]{2,1,0:T(4,128)(2,1)}), bf16[16,4,3584]{2,1,0:T(4,128)(2,1)S(1)}, u32[]{:S(2)}, u32[]{:S(2)}) async-start(bf16[16,4,3584]{2,1,0:T(4,128)(2,1)} %bitcast.77), calls=%async_computation | async-start | bytes 917504 | tf_op jit(solution)/shard_map/while/body/eval_jaxpr/all_to_all | solution.py:77
  20.0 0.7 compare_select_fusion.2
  20.8 0.7 fusion.73
  21.5 0.9 fusion.72
  22.5 10.5 %all-to-all-done = bf16[16,4,3584]{2,1,0:T(4,128)(2,1)S(1)} async-done(((bf16[16,4,3584]{2,1,0:T(4,128)(2,1)}), bf16[16,4,3584]{2,1,0:T(4,128)(2,1)S(1)}, u32[]{:S(2)}, u32[]{:S(2)}) %all-to-all-start) | async-done | bytes 458784 | tf_op jit(solution)/shard_map/while/body/eval_jaxpr/all_to_all | solution.py:77
  33.2 2.8 fusion.71
  35.9 4.6 %convolution_convert_fusion.5 = bf16[64,3584]{1,0:T(8,128)(2,1)S(1)} fusion(bf16[1,512,3584]{2,1,0:T(8,128)(2,1)} %get-tuple-element.450, bf16[64,3584]{1,0:T(8,128)(2,1)S(1)} %reshape.218, bf16[1,3584,512]{2,1,0:T(8,128)(2,1)} %get-tuple-element.449, f32[64,512]{1,0:T(8,128)S(1)} %fusion.71), kind=kOutput, calls=%fused_computation.1.clone.1 | convolution fusion | flops 470188032 | bytes 8388608 | tf_op jit(solution)/shard_map/while/body/eval_jaxpr/dot_general | solution.py:46
  40.6 0.9 reshape.219
  41.4 3.8 %all-to-all-start.1 = ((bf16[16,4,3584]{2,1,0:T(4,128)(2,1)}), bf16[16,4,3584]{2,1,0:T(4,128)(2,1)S(1)}, u32[]{:S(2)}, u32[]{:S(2)}) async-start(bf16[16,4,3584]{2,1,0:T(4,128)(2,1)} %reshape.219), calls=%async_computation.1 | async-start | bytes 917504 | tf_op jit(solution)/shard_map/while/body/eval_jaxpr/all_to_all | solution.py:49
  45.4 13.1 %all-to-all-done.1 = bf16[16,4,3584]{2,1,0:T(4,128)(2,1)S(1)} async-done(((bf16[16,4,3584]{2,1,0:T(4,128)(2,1)}), bf16[16,4,3584]{2,1,0:T(4,128)(2,1)S(1)}, u32[]{:S(2)}, u32[]{:S(2)}) %all-to-all-start.1) | async-done | bytes 458784 | tf_op jit(solution)/shard_map/while/body/eval_jaxpr/all_to_all | solution.py:49
  58.8 0.6 gather_fusion
  59.9 3.4 %collective-permute-start = (bf16[8,3584]{1,0:T(8,128)(2,1)S(1)}, bf16[8,3584]{1,0:T(8,128)(2,1)S(1)}, u32[]{:S(2)}, u32[]{:S(2)}) collective-permute-start(bf16[8,3584]{1,0:T(8,128)(2,1)S(1)} %get-tuple-element.401), channel_id=1, source_target_pairs={{0,16},{1,17},{2,18},{3,19},{4,20},{5,21},{6,22},{7,23},{8,24},{9,... | collective-permute-start | bytes 172040 | tf_op jit(solution)/shard_map/while/body/eval_jaxpr/ppermute | solution.py:12
  63.4 1.8 collective-permute-done
  65.2 0.7 constant_dynamic-slice_fusion.6
  66.5 0.7 multiply_add_fusion.2
  67.2 1.0 fusion.70
  68.2 0.8 reduce.2
  69.3 0.9 broadcast_in_dim.134
  70.1 3.8 %all-to-all-start = ((bf16[16,4,3584]{2,1,0:T(4,128)(2,1)}), bf16[16,4,3584]{2,1,0:T(4,128)(2,1)S(1)}, u32[]{:S(2)}, u32[]{:S(2)}) async-start(bf16[16,4,3584]{2,1,0:T(4,128)(2,1)} %bitcast.77), calls=%async_computation | async-start | bytes 917504 | tf_op jit(solution)/shard_map/while/body/eval_jaxpr/all_to_all | solution.py:77
  74.1 0.7 compare_select_fusion.2
  75.0 0.7 fusion.73
  75.6 0.9 fusion.72
  76.6 10.5 %all-to-all-done = bf16[16,4,3584]{2,1,0:T(4,128)(2,1)S(1)} async-done(((bf16[16,4,3584]{2,1,0:T(4,128)(2,1)}), bf16[16,4,3584]{2,1,0:T(4,128)(2,1)S(1)}, u32[]{:S(2)}, u32[]{:S(2)}) %all-to-all-start) | async-done | bytes 458784 | tf_op jit(solution)/shard_map/while/body/eval_jaxpr/all_to_all | solution.py:77
  87.3 2.8 fusion.71
  90.1 4.6 %convolution_convert_fusion.5 = bf16[64,3584]{1,0:T(8,128)(2,1)S(1)} fusion(bf16[1,512,3584]{2,1,0:T(8,128)(2,1)} %get-tuple-element.450, bf16[64,3584]{1,0:T(8,128)(2,1)S(1)} %reshape.218, bf16[1,3584,512]{2,1,0:T(8,128)(2,1)} %get-tuple-element.449, f32[64,512]{1,0:T(8,128)S(1)} %fusion.71), kind=kOutput, calls=%fused_computation.1.clone.1 | convolution fusion | flops 470188032 | bytes 8388608 | tf_op jit(solution)/shard_map/while/body/eval_jaxpr/dot_general | solution.py:46
  94.7 0.9 reshape.219
  95.6 3.8 %all-to-all-start.1 = ((bf16[16,4,3584]{2,1,0:T(4,128)(2,1)}), bf16[16,4,3584]{2,1,0:T(4,128)(2,1)S(1)}, u32[]{:S(2)}, u32[]{:S(2)}) async-start(bf16[16,4,3584]{2,1,0:T(4,128)(2,1)} %reshape.219), calls=%async_computation.1 | async-start | bytes 917504 | tf_op jit(solution)/shard_map/while/body/eval_jaxpr/all_to_all | solution.py:49
  99.5 13.1 %all-to-all-done.1 = bf16[16,4,3584]{2,1,0:T(4,128)(2,1)S(1)} async-done(((bf16[16,4,3584]{2,1,0:T(4,128)(2,1)}), bf16[16,4,3584]{2,1,0:T(4,128)(2,1)S(1)}, u32[]{:S(2)}, u32[]{:S(2)}) %all-to-all-start.1) | async-done | bytes 458784 | tf_op jit(solution)/shard_map/while/body/eval_jaxpr/all_to_all | solution.py:49
  112.9 0.6 gather_fusion
  114.1 4.3 %collective-permute-start = (bf16[8,3584]{1,0:T(8,128)(2,1)S(1)}, bf16[8,3584]{1,0:T(8,128)(2,1)S(1)}, u32[]{:S(2)}, u32[]{:S(2)}) collective-permute-start(bf16[8,3584]{1,0:T(8,128)(2,1)S(1)} %get-tuple-element.401), channel_id=1, source_target_pairs={{0,16},{1,17},{2,18},{3,19},{4,20},{5,21},{6,22},{7,23},{8,24},{9,... | collective-permute-start | bytes 172040 | tf_op jit(solution)/shard_map/while/body/eval_jaxpr/ppermute | solution.py:12
  118.4 1.8 collective-permute-done
  120.2 0.7 constant_dynamic-slice_fusion.6
  121.5 0.7 multiply_add_fusion.2
  122.3 1.0 fusion.70
  123.2 0.8 reduce.2
  124.3 0.9 broadcast_in_dim.134
  125.2 3.8 %all-to-all-start = ((bf16[16,4,3584]{2,1,0:T(4,128)(2,1)}), bf16[16,4,3584]{2,1,0:T(4,128)(2,1)S(1)}, u32[]{:S(2)}, u32[]{:S(2)}) async-start(bf16[16,4,3584]{2,1,0:T(4,128)(2,1)} %bitcast.77), calls=%async_computation | async-start | bytes 917504 | tf_op jit(solution)/shard_map/while/body/eval_jaxpr/all_to_all | solution.py:77
  129.1 0.7 compare_select_fusion.2
  130.0 0.7 fusion.73
  130.7 0.9 fusion.72
  131.7 10.5 %all-to-all-done = bf16[16,4,3584]{2,1,0:T(4,128)(2,1)S(1)} async-done(((bf16[16,4,3584]{2,1,0:T(4,128)(2,1)}), bf16[16,4,3584]{2,1,0:T(4,128)(2,1)S(1)}, u32[]{:S(2)}, u32[]{:S(2)}) %all-to-all-start) | async-done | bytes 458784 | tf_op jit(solution)/shard_map/while/body/eval_jaxpr/all_to_all | solution.py:77
  142.3 2.8 fusion.71
  145.1 4.6 %convolution_convert_fusion.5 = bf16[64,3584]{1,0:T(8,128)(2,1)S(1)} fusion(bf16[1,512,3584]{2,1,0:T(8,128)(2,1)} %get-tuple-element.450, bf16[64,3584]{1,0:T(8,128)(2,1)S(1)} %reshape.218, bf16[1,3584,512]{2,1,0:T(8,128)(2,1)} %get-tuple-element.449, f32[64,512]{1,0:T(8,128)S(1)} %fusion.71), kind=kOutput, calls=%fused_computation.1.clone.1 | convolution fusion | flops 470188032 | bytes 8388608 | tf_op jit(solution)/shard_map/while/body/eval_jaxpr/dot_general | solution.py:46
  149.7 0.9 reshape.219
  150.6 3.8 %all-to-all-start.1 = ((bf16[16,4,3584]{2,1,0:T(4,128)(2,1)}), bf16[16,4,3584]{2,1,0:T(4,128)(2,1)S(1)}, u32[]{:S(2)}, u32[]{:S(2)}) async-start(bf16[16,4,3584]{2,1,0:T(4,128)(2,1)} %reshape.219), calls=%async_computation.1 | async-start | bytes 917504 | tf_op jit(solution)/shard_map/while/body/eval_jaxpr/all_to_all | solution.py:49
  154.5 13.1 %all-to-all-done.1 = bf16[16,4,3584]{2,1,0:T(4,128)(2,1)S(1)} async-done(((bf16[16,4,3584]{2,1,0:T(4,128)(2,1)}), bf16[16,4,3584]{2,1,0:T(4,128)(2,1)S(1)}, u32[]{:S(2)}, u32[]{:S(2)}) %all-to-all-start.1) | async-done | bytes 458784 | tf_op jit(solution)/shard_map/while/body/eval_jaxpr/all_to_all | solution.py:49
  167.9 0.6 gather_fusion
  169.1 4.3 %collective-permute-start = (bf16[8,3584]{1,0:T(8,128)(2,1)S(1)}, bf16[8,3584]{1,0:T(8,128)(2,1)S(1)}, u32[]{:S(2)}, u32[]{:S(2)}) collective-permute-start(bf16[8,3584]{1,0:T(8,128)(2,1)S(1)} %get-tuple-element.401), channel_id=1, source_target_pairs={{0,16},{1,17},{2,18},{3,19},{4,20},{5,21},{6,22},{7,23},{8,24},{9,... | collective-permute-start | bytes 172040 | tf_op jit(solution)/shard_map/while/body/eval_jaxpr/ppermute | solution.py:12
  173.4 1.8 collective-permute-done
  175.2 0.6 broadcast_select_fusion
  175.9 21.4 %all-reduce.3.cloned.1.call-done = bf16[2,8,3584]{2,1,0:T(8,128)(2,1)} async-done(((bf16[2,8,3584]{2,1,0:T(8,128)(2,1)}), bf16[2,8,3584]{2,1,0:T(8,128)(2,1)}) %all-reduce.3.cloned.1.call-update) | async-done | bytes 114704 | tf_op jit(solution)/shard_map/psum | solution.py:17
  197.5 42.9 %all-gather.2.cloned.1.call-done = bf16[2,128,3584]{2,1,0:T(8,128)(2,1)} async-done(((bf16[2,8,3584]{2,1,0:T(8,128)(2,1)}), bf16[2,128,3584]{2,1,0:T(8,128)(2,1)}) %all-gather.2.cloned.1.call-update) | async-done | bytes 1835024 | tf_op jit(solution)/shard_map/all_gather | solution.py:110
  240.4 1.9 fusion.30
  242.4 2.3 fusion.39
  244.6 38.4 %pmax.7 = f32[2,128]{1,0:T(2,128)S(1)} all-reduce(f32[2,128]{1,0:T(2,128)S(1)} %get-tuple-element.314), channel_id=1, replica_groups=mesh['section'=2,'expert'=16] {'section','expert'}, use_global_device_ids=true, to_apply=%region_15.16 | all-reduce | flops 256 | bytes 2048 | tf_op jit(solution)/shard_map/pmax | solution.py:120
  283.3 40.9 %all-reduce = (f32[2,128]{1,0:T(2,128)S(1)}, f32[2,128]{1,0:T(2,128)S(1)}) all-reduce(f32[2,128]{1,0:T(2,128)S(1)} %get-tuple-element.279, f32[2,128]{1,0:T(2,128)S(1)} %get-tuple-element.278), channel_id=1, replica_groups=mesh['section'=2,'expert'=16] {'section','expert'}, use_global_device_ids=true, to_apply=%region_13.14 | all-reduce | flops 512 | bytes 4096 | tf_op jit(solution)/shard_map/psum | solution.py:122
  324.3 0.6 constant_dynamic-slice_fusion.2
  324.9 0.6 div.62
  (100 shorter events, 7.7 us)
Async XLA Ops:
  7.2 235.2 %copy-start = (bf16[256,3584]{1,0:T(8,128)(2,1)S(1)}, bf16[256,3584]{1,0:T(8,128)(2,1)}, u32[]{:S(2)}) copy-start(bf16[256,3584]{1,0:T(8,128)(2,1)} %param.20) | copy-start | bytes 5505028
  7.2 190.2 %all-reduce.3.cloned.1.call-start = ((), (), s32[]{:S(2)}) async-start(), calls=%async_computation.2 | async-start | bytes 229376 | tf_op jit(solution)/shard_map/psum | solution.py:17
  7.3 235.1 %copy-start.3 = (f32[3584]{0:T(1024)S(1)}, f32[3584]{0:T(1024)}, u32[]{:S(2)}) copy-start(f32[3584]{0:T(1024)} %param.19) | copy-start | bytes 43012
  12.4 20.6 %all-to-all-start = ((bf16[16,4,3584]{2,1,0:T(4,128)(2,1)}), bf16[16,4,3584]{2,1,0:T(4,128)(2,1)S(1)}, u32[]{:S(2)}, u32[]{:S(2)}) async-start(bf16[16,4,3584]{2,1,0:T(4,128)(2,1)} %bitcast.77), calls=%async_computation | async-start | bytes 917504 | tf_op jit(solution)/shard_map/while/body/eval_jaxpr/all_to_all | solution.py:77
  41.4 17.0 %all-to-all-start.1 = ((bf16[16,4,3584]{2,1,0:T(4,128)(2,1)}), bf16[16,4,3584]{2,1,0:T(4,128)(2,1)S(1)}, u32[]{:S(2)}, u32[]{:S(2)}) async-start(bf16[16,4,3584]{2,1,0:T(4,128)(2,1)} %reshape.219), calls=%async_computation.1 | async-start | bytes 917504 | tf_op jit(solution)/shard_map/while/body/eval_jaxpr/all_to_all | solution.py:49
  59.9 5.2 %collective-permute-start = (bf16[8,3584]{1,0:T(8,128)(2,1)S(1)}, bf16[8,3584]{1,0:T(8,128)(2,1)S(1)}, u32[]{:S(2)}, u32[]{:S(2)}) collective-permute-start(bf16[8,3584]{1,0:T(8,128)(2,1)S(1)} %get-tuple-element.401), channel_id=1, source_target_pairs={{0,16},{1,17},{2,18},{3,19},{4,20},{5,21},{6,22},{7,23},{8,24},{9,... | collective-permute-start | bytes 172040 | tf_op jit(solution)/shard_map/while/body/eval_jaxpr/ppermute | solution.py:12
  70.1 17.0 %all-to-all-start = ((bf16[16,4,3584]{2,1,0:T(4,128)(2,1)}), bf16[16,4,3584]{2,1,0:T(4,128)(2,1)S(1)}, u32[]{:S(2)}, u32[]{:S(2)}) async-start(bf16[16,4,3584]{2,1,0:T(4,128)(2,1)} %bitcast.77), calls=%async_computation | async-start | bytes 917504 | tf_op jit(solution)/shard_map/while/body/eval_jaxpr/all_to_all | solution.py:77
  95.6 17.0 %all-to-all-start.1 = ((bf16[16,4,3584]{2,1,0:T(4,128)(2,1)}), bf16[16,4,3584]{2,1,0:T(4,128)(2,1)S(1)}, u32[]{:S(2)}, u32[]{:S(2)}) async-start(bf16[16,4,3584]{2,1,0:T(4,128)(2,1)} %reshape.219), calls=%async_computation.1 | async-start | bytes 917504 | tf_op jit(solution)/shard_map/while/body/eval_jaxpr/all_to_all | solution.py:49
  114.1 6.1 %collective-permute-start = (bf16[8,3584]{1,0:T(8,128)(2,1)S(1)}, bf16[8,3584]{1,0:T(8,128)(2,1)S(1)}, u32[]{:S(2)}, u32[]{:S(2)}) collective-permute-start(bf16[8,3584]{1,0:T(8,128)(2,1)S(1)} %get-tuple-element.401), channel_id=1, source_target_pairs={{0,16},{1,17},{2,18},{3,19},{4,20},{5,21},{6,22},{7,23},{8,24},{9,... | collective-permute-start | bytes 172040 | tf_op jit(solution)/shard_map/while/body/eval_jaxpr/ppermute | solution.py:12
  125.2 17.0 %all-to-all-start = ((bf16[16,4,3584]{2,1,0:T(4,128)(2,1)}), bf16[16,4,3584]{2,1,0:T(4,128)(2,1)S(1)}, u32[]{:S(2)}, u32[]{:S(2)}) async-start(bf16[16,4,3584]{2,1,0:T(4,128)(2,1)} %bitcast.77), calls=%async_computation | async-start | bytes 917504 | tf_op jit(solution)/shard_map/while/body/eval_jaxpr/all_to_all | solution.py:77
  150.6 17.0 %all-to-all-start.1 = ((bf16[16,4,3584]{2,1,0:T(4,128)(2,1)}), bf16[16,4,3584]{2,1,0:T(4,128)(2,1)S(1)}, u32[]{:S(2)}, u32[]{:S(2)}) async-start(bf16[16,4,3584]{2,1,0:T(4,128)(2,1)} %reshape.219), calls=%async_computation.1 | async-start | bytes 917504 | tf_op jit(solution)/shard_map/while/body/eval_jaxpr/all_to_all | solution.py:49
  169.1 6.1 %collective-permute-start = (bf16[8,3584]{1,0:T(8,128)(2,1)S(1)}, bf16[8,3584]{1,0:T(8,128)(2,1)S(1)}, u32[]{:S(2)}, u32[]{:S(2)}) collective-permute-start(bf16[8,3584]{1,0:T(8,128)(2,1)S(1)} %get-tuple-element.401), channel_id=1, source_target_pairs={{0,16},{1,17},{2,18},{3,19},{4,20},{5,21},{6,22},{7,23},{8,24},{9,... | collective-permute-start | bytes 172040 | tf_op jit(solution)/shard_map/while/body/eval_jaxpr/ppermute | solution.py:12
  175.9 64.5 %all-gather.2.cloned.1.call-start = ((), (), s32[]{:S(2)}) async-start(), calls=%async_computation.3 | async-start | bytes 1949696 | tf_op jit(solution)/shard_map/all_gather | solution.py:110
  197.4 85.6 %copy-start.1 = (s32[2,128]{1,0:T(2,128)S(1)}, s32[2,128]{1,0:T(2,128)}, u32[]{:S(2)}) copy-start(s32[2,128]{1,0:T(2,128)} %param.22) | copy-start | bytes 3076
  197.4 126.7 %copy-start.2 = (s32[2,128]{1,0:T(2,128)S(1)}, s32[2,128]{1,0:T(2,128)}, u32[]{:S(2)}) copy-start(s32[2,128]{1,0:T(2,128)} %param.23) | copy-start | bytes 3076
Sparse Core Ops, SparseCore 0:
  176.0 21.3 all-reduce.2
  199.7 40.6 all-gather.1
where the time goes:
time: 334 us; the launch traced here: 332 us
  waiting for transfers between devices  141 us (42%)
  blocking collectives  79.3 us (24%)
  starting transfers between devices  38.5 us (12%)
  matrix products  28 us (8%)
  other arithmetic  16 us (5%)
  local copies, waits for them, and re-layouts  15.4 us (5%)
  between operations  14.1 us (4%)
    all_gather x1, waiting for transfers between devices, body(): lax.all_gather(shared, 'expert', axis=1, tiled=True)  42.9 us
    psum x1, blocking collectives, body(): lax.psum((local_sum, target_part), ('section', 'expert'))  40.9 us
    all_to_all x3, waiting for transfers between devices, expert_rows(): lax.all_to_all(partial_value.reshape(sources, slot_count, width_in), 'exp...  39.2 us
    pmax x1, blocking collectives, body(): peak = lax.pmax(local_max, ('section', 'expert'))  38.4 us
    all_to_all x3, waiting for transfers between devices, expert_layer(): lax.all_to_all(outgoing, 'expert', split_axis=0, concat_axis=0, tiled=True)  31.6 us
    psum x1, waiting for transfers between devices, broadcast(): return lax.psum(block, axis)  21.4 us
    all_to_all x3, starting transfers between devices, expert_layer(): lax.all_to_all(outgoing, 'expert', split_axis=0, concat_axis=0, tiled=True)  15 us
    dot_general x3, matrix products, expert_rows(): jnp.dot(inner, w_down[0], preferred_element_type=jnp.float32)  13.8 us
  transfers between devices with their start and end apart: 11, of which 11 were waited for; matrix products, arithmetic and copies ran while one was open for 3% of the time, Pallas kernels for 0%

commit v1 on v0

--- a/solution.py
+++ b/solution.py
@@ -14,7 +14,7 @@
 
 def broadcast(block, axis, holder):
     block = jnp.where(lax.axis_index(axis) == holder, block, jnp.zeros_like(block))
-    return lax.psum(block, axis)
+    return jnp.sum(lax.all_gather(block, axis), axis=0)
 
 
 def rms_scale(states, gain):

time: 334 us -> 316 us (0.946)
  waiting for transfers between devices: 141 us -> 117 us
  blocking collectives: 79.3 us -> 85.1 us
    psum x1 -> x0, waiting for transfers between devices: 21.4 us -> none  [broadcast(): return lax.psum(block, axis)]
    all_gather x0 -> x1, blocking collectives: none -> 5.78 us  [broadcast(): return jnp.sum(lax.all_gather(block, axis), axis=0)]
  transfers between devices with their start and end apart: 11 -> 10, of which waited for: 11 -> 10; matrix products, arithmetic and copies ran while one was open for 3% -> 3% of each run, Pallas kernels for 0% -> 0%
where the time goes in v1:
time: 316 us; the launch traced here: 314 us
  waiting for transfers between devices  117 us (37%)
  blocking collectives  85.1 us (27%)
  starting transfers between devices  38.4 us (12%)
  matrix products  28 us (9%)
  other arithmetic  16 us (5%)
  local copies, waits for them, and re-layouts  15.4 us (5%)
  between operations  14.1 us (4%)
    psum x1, blocking collectives, body(): lax.psum((local_sum, target_part), ('section', 'expert'))  40.9 us
    all_gather x1, waiting for transfers between devices, body(): lax.all_gather(shared, 'expert', axis=1, tiled=True)  40.5 us
    all_to_all x3, waiting for transfers between devices, expert_rows(): lax.all_to_all(partial_value.reshape(sources, slot_count, width_in), 'exp...  39.2 us
    pmax x1, blocking collectives, body(): peak = lax.pmax(local_max, ('section', 'expert'))  38.4 us
    all_to_all x3, waiting for transfers between devices, expert_layer(): lax.all_to_all(outgoing, 'expert', split_axis=0, concat_axis=0, tiled=True)  31.6 us
    all_to_all x3, starting transfers between devices, expert_layer(): lax.all_to_all(outgoing, 'expert', split_axis=0, concat_axis=0, tiled=True)  15 us
    dot_general x3, matrix products, expert_rows(): jnp.dot(inner, w_down[0], preferred_element_type=jnp.float32)  13.8 us
    ppermute x3, starting transfers between devices, shifted(): return lax.ppermute(shard, axis, pairs)  12 us
  transfers between devices with their start and end apart: 10, of which 10 were waited for; matrix products, arithmetic and copies ran while one was open for 3% of the time, Pallas kernels for 0%

profile of v1, /device:TPU:0, one launch (start us, length us, event | category | flops | bytes accessed | tf_op | source)
XLA Modules:
  0.0 314.2 jit_solution(8278069994854709827)
XLA Ops:
  7.3 167.9 %while.17 = (s32[]{:T(128)}, bf16[8,3584]{1,0:T(8,128)(2,1)S(1)}, bf16[2,8,3584]{2,1,0:T(8,128)(2,1)S(1)}, pred[]{:T(512)}, bf16[2,8,3584]{2,1,0:T(8,128)(2,1)},...) while((s32[]{:T(128)}, bf16[8,3584]{1,0:T(8,128)(2,1)S(1)}, ...), condition=%wide.region_9.10_spmd, body=%wide.region_0.9_spmd.sunk | while | flops 707251328 | bytes 21631636 | solution.py:108
  7.3 0.8 constant_dynamic-slice_fusion.6
  8.7 0.7 multiply_add_fusion.2
  9.5 1.0 fusion.70
  10.5 0.8 reduce.3
  11.5 0.9 broadcast_in_dim.134
  12.4 7.4 %all-to-all-start = ((bf16[16,4,3584]{2,1,0:T(4,128)(2,1)}), bf16[16,4,3584]{2,1,0:T(4,128)(2,1)S(1)}, u32[]{:S(2)}, u32[]{:S(2)}) async-start(bf16[16,4,3584]{2,1,0:T(4,128)(2,1)} %bitcast.78), calls=%async_computation | async-start | bytes 917504 | tf_op jit(solution)/shard_map/while/body/eval_jaxpr/all_to_all | solution.py:77
  20.0 0.7 compare_select_fusion.2
  20.8 0.7 fusion.73
  21.5 0.9 fusion.72
  22.5 10.5 %all-to-all-done = bf16[16,4,3584]{2,1,0:T(4,128)(2,1)S(1)} async-done(((bf16[16,4,3584]{2,1,0:T(4,128)(2,1)}), bf16[16,4,3584]{2,1,0:T(4,128)(2,1)S(1)}, u32[]{:S(2)}, u32[]{:S(2)}) %all-to-all-start) | async-done | bytes 458784 | tf_op jit(solution)/shard_map/while/body/eval_jaxpr/all_to_all | solution.py:77
  33.2 2.8 fusion.71
  35.9 4.6 %convolution_convert_fusion.5 = bf16[64,3584]{1,0:T(8,128)(2,1)S(1)} fusion(bf16[1,512,3584]{2,1,0:T(8,128)(2,1)} %get-tuple-element.450, bf16[64,3584]{1,0:T(8,128)(2,1)S(1)} %reshape.219, bf16[1,3584,512]{2,1,0:T(8,128)(2,1)} %get-tuple-element.449, f32[64,512]{1,0:T(8,128)S(1)} %fusion.71), kind=kOutput, calls=%fused_computation.1.clone.1 | convolution fusion | flops 470188032 | bytes 8388608 | tf_op jit(solution)/shard_map/while/body/eval_jaxpr/dot_general | solution.py:46
  40.6 0.9 reshape.220
  41.4 3.8 %all-to-all-start.1 = ((bf16[16,4,3584]{2,1,0:T(4,128)(2,1)}), bf16[16,4,3584]{2,1,0:T(4,128)(2,1)S(1)}, u32[]{:S(2)}, u32[]{:S(2)}) async-start(bf16[16,4,3584]{2,1,0:T(4,128)(2,1)} %reshape.220), calls=%async_computation.1 | async-start | bytes 917504 | tf_op jit(solution)/shard_map/while/body/eval_jaxpr/all_to_all | solution.py:49
  45.4 13.1 %all-to-all-done.1 = bf16[16,4,3584]{2,1,0:T(4,128)(2,1)S(1)} async-done(((bf16[16,4,3584]{2,1,0:T(4,128)(2,1)}), bf16[16,4,3584]{2,1,0:T(4,128)(2,1)S(1)}, u32[]{:S(2)}, u32[]{:S(2)}) %all-to-all-start.1) | async-done | bytes 458784 | tf_op jit(solution)/shard_map/while/body/eval_jaxpr/all_to_all | solution.py:49
  58.8 0.6 gather_fusion
  59.9 3.4 %collective-permute-start = (bf16[8,3584]{1,0:T(8,128)(2,1)S(1)}, bf16[8,3584]{1,0:T(8,128)(2,1)S(1)}, u32[]{:S(2)}, u32[]{:S(2)}) collective-permute-start(bf16[8,3584]{1,0:T(8,128)(2,1)S(1)} %get-tuple-element.401), channel_id=1, source_target_pairs={{0,16},{1,17},{2,18},{3,19},{4,20},{5,21},{6,22},{7,23},{8,24},{9,... | collective-permute-start | bytes 172040 | tf_op jit(solution)/shard_map/while/body/eval_jaxpr/ppermute | solution.py:12
  63.4 1.8 collective-permute-done
  65.2 0.7 constant_dynamic-slice_fusion.6
  66.5 0.7 multiply_add_fusion.2
  67.2 1.0 fusion.70
  68.2 0.8 reduce.3
  69.3 0.9 broadcast_in_dim.134
  70.1 3.8 %all-to-all-start = ((bf16[16,4,3584]{2,1,0:T(4,128)(2,1)}), bf16[16,4,3584]{2,1,0:T(4,128)(2,1)S(1)}, u32[]{:S(2)}, u32[]{:S(2)}) async-start(bf16[16,4,3584]{2,1,0:T(4,128)(2,1)} %bitcast.78), calls=%async_computation | async-start | bytes 917504 | tf_op jit(solution)/shard_map/while/body/eval_jaxpr/all_to_all | solution.py:77
  74.1 0.7 compare_select_fusion.2
  75.0 0.7 fusion.73
  75.6 0.9 fusion.72
  76.6 10.5 %all-to-all-done = bf16[16,4,3584]{2,1,0:T(4,128)(2,1)S(1)} async-done(((bf16[16,4,3584]{2,1,0:T(4,128)(2,1)}), bf16[16,4,3584]{2,1,0:T(4,128)(2,1)S(1)}, u32[]{:S(2)}, u32[]{:S(2)}) %all-to-all-start) | async-done | bytes 458784 | tf_op jit(solution)/shard_map/while/body/eval_jaxpr/all_to_all | solution.py:77
  87.3 2.8 fusion.71
  90.1 4.6 %convolution_convert_fusion.5 = bf16[64,3584]{1,0:T(8,128)(2,1)S(1)} fusion(bf16[1,512,3584]{2,1,0:T(8,128)(2,1)} %get-tuple-element.450, bf16[64,3584]{1,0:T(8,128)(2,1)S(1)} %reshape.219, bf16[1,3584,512]{2,1,0:T(8,128)(2,1)} %get-tuple-element.449, f32[64,512]{1,0:T(8,128)S(1)} %fusion.71), kind=kOutput, calls=%fused_computation.1.clone.1 | convolution fusion | flops 470188032 | bytes 8388608 | tf_op jit(solution)/shard_map/while/body/eval_jaxpr/dot_general | solution.py:46
  94.7 0.9 reshape.220
  95.6 3.8 %all-to-all-start.1 = ((bf16[16,4,3584]{2,1,0:T(4,128)(2,1)}), bf16[16,4,3584]{2,1,0:T(4,128)(2,1)S(1)}, u32[]{:S(2)}, u32[]{:S(2)}) async-start(bf16[16,4,3584]{2,1,0:T(4,128)(2,1)} %reshape.220), calls=%async_computation.1 | async-start | bytes 917504 | tf_op jit(solution)/shard_map/while/body/eval_jaxpr/all_to_all | solution.py:49
  99.5 13.1 %all-to-all-done.1 = bf16[16,4,3584]{2,1,0:T(4,128)(2,1)S(1)} async-done(((bf16[16,4,3584]{2,1,0:T(4,128)(2,1)}), bf16[16,4,3584]{2,1,0:T(4,128)(2,1)S(1)}, u32[]{:S(2)}, u32[]{:S(2)}) %all-to-all-start.1) | async-done | bytes 458784 | tf_op jit(solution)/shard_map/while/body/eval_jaxpr/all_to_all | solution.py:49
  112.9 0.6 gather_fusion
  114.1 4.3 %collective-permute-start = (bf16[8,3584]{1,0:T(8,128)(2,1)S(1)}, bf16[8,3584]{1,0:T(8,128)(2,1)S(1)}, u32[]{:S(2)}, u32[]{:S(2)}) collective-permute-start(bf16[8,3584]{1,0:T(8,128)(2,1)S(1)} %get-tuple-element.401), channel_id=1, source_target_pairs={{0,16},{1,17},{2,18},{3,19},{4,20},{5,21},{6,22},{7,23},{8,24},{9,... | collective-permute-start | bytes 172040 | tf_op jit(solution)/shard_map/while/body/eval_jaxpr/ppermute | solution.py:12
  118.4 1.8 collective-permute-done
  120.2 0.7 constant_dynamic-slice_fusion.6
  121.5 0.7 multiply_add_fusion.2
  122.3 1.0 fusion.70
  123.2 0.8 reduce.3
  124.3 0.9 broadcast_in_dim.134
  125.2 3.8 %all-to-all-start = ((bf16[16,4,3584]{2,1,0:T(4,128)(2,1)}), bf16[16,4,3584]{2,1,0:T(4,128)(2,1)S(1)}, u32[]{:S(2)}, u32[]{:S(2)}) async-start(bf16[16,4,3584]{2,1,0:T(4,128)(2,1)} %bitcast.78), calls=%async_computation | async-start | bytes 917504 | tf_op jit(solution)/shard_map/while/body/eval_jaxpr/all_to_all | solution.py:77
  129.1 0.7 compare_select_fusion.2
  130.0 0.7 fusion.73
  130.7 0.9 fusion.72
  131.7 10.5 %all-to-all-done = bf16[16,4,3584]{2,1,0:T(4,128)(2,1)S(1)} async-done(((bf16[16,4,3584]{2,1,0:T(4,128)(2,1)}), bf16[16,4,3584]{2,1,0:T(4,128)(2,1)S(1)}, u32[]{:S(2)}, u32[]{:S(2)}) %all-to-all-start) | async-done | bytes 458784 | tf_op jit(solution)/shard_map/while/body/eval_jaxpr/all_to_all | solution.py:77
  142.3 2.8 fusion.71
  145.1 4.6 %convolution_convert_fusion.5 = bf16[64,3584]{1,0:T(8,128)(2,1)S(1)} fusion(bf16[1,512,3584]{2,1,0:T(8,128)(2,1)} %get-tuple-element.450, bf16[64,3584]{1,0:T(8,128)(2,1)S(1)} %reshape.219, bf16[1,3584,512]{2,1,0:T(8,128)(2,1)} %get-tuple-element.449, f32[64,512]{1,0:T(8,128)S(1)} %fusion.71), kind=kOutput, calls=%fused_computation.1.clone.1 | convolution fusion | flops 470188032 | bytes 8388608 | tf_op jit(solution)/shard_map/while/body/eval_jaxpr/dot_general | solution.py:46
  149.7 0.9 reshape.220
  150.6 3.8 %all-to-all-start.1 = ((bf16[16,4,3584]{2,1,0:T(4,128)(2,1)}), bf16[16,4,3584]{2,1,0:T(4,128)(2,1)S(1)}, u32[]{:S(2)}, u32[]{:S(2)}) async-start(bf16[16,4,3584]{2,1,0:T(4,128)(2,1)} %reshape.220), calls=%async_computation.1 | async-start | bytes 917504 | tf_op jit(solution)/shard_map/while/body/eval_jaxpr/all_to_all | solution.py:49
  154.5 13.1 %all-to-all-done.1 = bf16[16,4,3584]{2,1,0:T(4,128)(2,1)S(1)} async-done(((bf16[16,4,3584]{2,1,0:T(4,128)(2,1)}), bf16[16,4,3584]{2,1,0:T(4,128)(2,1)S(1)}, u32[]{:S(2)}, u32[]{:S(2)}) %all-to-all-start.1) | async-done | bytes 458784 | tf_op jit(solution)/shard_map/while/body/eval_jaxpr/all_to_all | solution.py:49
  167.9 0.6 gather_fusion
  169.1 4.3 %collective-permute-start = (bf16[8,3584]{1,0:T(8,128)(2,1)S(1)}, bf16[8,3584]{1,0:T(8,128)(2,1)S(1)}, u32[]{:S(2)}, u32[]{:S(2)}) collective-permute-start(bf16[8,3584]{1,0:T(8,128)(2,1)S(1)} %get-tuple-element.401), channel_id=1, source_target_pairs={{0,16},{1,17},{2,18},{3,19},{4,20},{5,21},{6,22},{7,23},{8,24},{9,... | collective-permute-start | bytes 172040 | tf_op jit(solution)/shard_map/while/body/eval_jaxpr/ppermute | solution.py:12
  173.4 1.8 collective-permute-done
  175.2 5.8 %all-gather = bf16[4,8,3584]{2,1,0:T(8,128)(2,1)S(1)} all-gather(bf16[2,8,3584]{2,1,0:T(8,128)(2,1)S(1)} %broadcast_select_fusion), channel_id=2, replica_groups=mesh['section'=2,'expert'=16] {'section'}, dimensions={0}, use_global_device_ids=true | all-gather | bytes 344064 | tf_op jit(solution)/shard_map/all_gather | solution.py:17
  181.0 0.7 reduce_sum.153
  181.8 40.5 %all-gather.3.cloned.1.call-done = bf16[2,128,3584]{2,1,0:T(8,128)(2,1)} async-done(((bf16[2,8,3584]{2,1,0:T(8,128)(2,1)}), bf16[2,128,3584]{2,1,0:T(8,128)(2,1)}) %all-gather.3.cloned.1.call-update) | async-done | bytes 1835024 | tf_op jit(solution)/shard_map/all_gather | solution.py:110
  222.2 1.9 fusion.30
  224.2 2.3 fusion.39
  226.5 38.4 %pmax.7 = f32[2,128]{1,0:T(2,128)S(1)} all-reduce(f32[2,128]{1,0:T(2,128)S(1)} %get-tuple-element.314), channel_id=1, replica_groups=mesh['section'=2,'expert'=16] {'section','expert'}, use_global_device_ids=true, to_apply=%region_15.16 | all-reduce | flops 256 | bytes 2048 | tf_op jit(solution)/shard_map/pmax | solution.py:120
  265.1 40.9 %all-reduce = (f32[2,128]{1,0:T(2,128)S(1)}, f32[2,128]{1,0:T(2,128)S(1)}) all-reduce(f32[2,128]{1,0:T(2,128)S(1)} %get-tuple-element.279, f32[2,128]{1,0:T(2,128)S(1)} %get-tuple-element.278), channel_id=1, replica_groups=mesh['section'=2,'expert'=16] {'section','expert'}, use_global_device_ids=true, to_apply=%region_13.14 | all-reduce | flops 512 | bytes 4096 | tf_op jit(solution)/shard_map/psum | solution.py:122
  306.1 0.6 constant_dynamic-slice_fusion.2
  306.7 0.6 div.62
  (99 shorter events, 7.7 us)
Async XLA Ops:
  7.2 217.0 %copy-start = (bf16[256,3584]{1,0:T(8,128)(2,1)S(1)}, bf16[256,3584]{1,0:T(8,128)(2,1)}, u32[]{:S(2)}) copy-start(bf16[256,3584]{1,0:T(8,128)(2,1)} %param.20) | copy-start | bytes 5505028
  7.2 215.1 %all-gather.3.cloned.1.call-start = ((), (), s32[]{:S(2)}) async-start(), calls=%async_computation.2 | async-start | bytes 1949696 | tf_op jit(solution)/shard_map/all_gather | solution.py:110
  7.3 216.9 %copy-start.3 = (f32[3584]{0:T(1024)S(1)}, f32[3584]{0:T(1024)}, u32[]{:S(2)}) copy-start(f32[3584]{0:T(1024)} %param.19) | copy-start | bytes 43012
  12.4 20.6 %all-to-all-start = ((bf16[16,4,3584]{2,1,0:T(4,128)(2,1)}), bf16[16,4,3584]{2,1,0:T(4,128)(2,1)S(1)}, u32[]{:S(2)}, u32[]{:S(2)}) async-start(bf16[16,4,3584]{2,1,0:T(4,128)(2,1)} %bitcast.78), calls=%async_computation | async-start | bytes 917504 | tf_op jit(solution)/shard_map/while/body/eval_jaxpr/all_to_all | solution.py:77
  41.4 17.0 %all-to-all-start.1 = ((bf16[16,4,3584]{2,1,0:T(4,128)(2,1)}), bf16[16,4,3584]{2,1,0:T(4,128)(2,1)S(1)}, u32[]{:S(2)}, u32[]{:S(2)}) async-start(bf16[16,4,3584]{2,1,0:T(4,128)(2,1)} %reshape.220), calls=%async_computation.1 | async-start | bytes 917504 | tf_op jit(solution)/shard_map/while/body/eval_jaxpr/all_to_all | solution.py:49
  59.9 5.2 %collective-permute-start = (bf16[8,3584]{1,0:T(8,128)(2,1)S(1)}, bf16[8,3584]{1,0:T(8,128)(2,1)S(1)}, u32[]{:S(2)}, u32[]{:S(2)}) collective-permute-start(bf16[8,3584]{1,0:T(8,128)(2,1)S(1)} %get-tuple-element.401), channel_id=1, source_target_pairs={{0,16},{1,17},{2,18},{3,19},{4,20},{5,21},{6,22},{7,23},{8,24},{9,... | collective-permute-start | bytes 172040 | tf_op jit(solution)/shard_map/while/body/eval_jaxpr/ppermute | solution.py:12
  70.1 17.0 %all-to-all-start = ((bf16[16,4,3584]{2,1,0:T(4,128)(2,1)}), bf16[16,4,3584]{2,1,0:T(4,128)(2,1)S(1)}, u32[]{:S(2)}, u32[]{:S(2)}) async-start(bf16[16,4,3584]{2,1,0:T(4,128)(2,1)} %bitcast.78), calls=%async_computation | async-start | bytes 917504 | tf_op jit(solution)/shard_map/while/body/eval_jaxpr/all_to_all | solution.py:77
  95.6 17.0 %all-to-all-start.1 = ((bf16[16,4,3584]{2,1,0:T(4,128)(2,1)}), bf16[16,4,3584]{2,1,0:T(4,128)(2,1)S(1)}, u32[]{:S(2)}, u32[]{:S(2)}) async-start(bf16[16,4,3584]{2,1,0:T(4,128)(2,1)} %reshape.220), calls=%async_computation.1 | async-start | bytes 917504 | tf_op jit(solution)/shard_map/while/body/eval_jaxpr/all_to_all | solution.py:49
  114.1 6.1 %collective-permute-start = (bf16[8,3584]{1,0:T(8,128)(2,1)S(1)}, bf16[8,3584]{1,0:T(8,128)(2,1)S(1)}, u32[]{:S(2)}, u32[]{:S(2)}) collective-permute-start(bf16[8,3584]{1,0:T(8,128)(2,1)S(1)} %get-tuple-element.401), channel_id=1, source_target_pairs={{0,16},{1,17},{2,18},{3,19},{4,20},{5,21},{6,22},{7,23},{8,24},{9,... | collective-permute-start | bytes 172040 | tf_op jit(solution)/shard_map/while/body/eval_jaxpr/ppermute | solution.py:12
  125.2 17.0 %all-to-all-start = ((bf16[16,4,3584]{2,1,0:T(4,128)(2,1)}), bf16[16,4,3584]{2,1,0:T(4,128)(2,1)S(1)}, u32[]{:S(2)}, u32[]{:S(2)}) async-start(bf16[16,4,3584]{2,1,0:T(4,128)(2,1)} %bitcast.78), calls=%async_computation | async-start | bytes 917504 | tf_op jit(solution)/shard_map/while/body/eval_jaxpr/all_to_all | solution.py:77
  150.6 17.0 %all-to-all-start.1 = ((bf16[16,4,3584]{2,1,0:T(4,128)(2,1)}), bf16[16,4,3584]{2,1,0:T(4,128)(2,1)S(1)}, u32[]{:S(2)}, u32[]{:S(2)}) async-start(bf16[16,4,3584]{2,1,0:T(4,128)(2,1)} %reshape.220), calls=%async_computation.1 | async-start | bytes 917504 | tf_op jit(solution)/shard_map/while/body/eval_jaxpr/all_to_all | solution.py:49
  169.1 6.1 %collective-permute-start = (bf16[8,3584]{1,0:T(8,128)(2,1)S(1)}, bf16[8,3584]{1,0:T(8,128)(2,1)S(1)}, u32[]{:S(2)}, u32[]{:S(2)}) collective-permute-start(bf16[8,3584]{1,0:T(8,128)(2,1)S(1)} %get-tuple-element.401), channel_id=1, source_target_pairs={{0,16},{1,17},{2,18},{3,19},{4,20},{5,21},{6,22},{7,23},{8,24},{9,... | collective-permute-start | bytes 172040 | tf_op jit(solution)/shard_map/while/body/eval_jaxpr/ppermute | solution.py:12
  181.7 83.1 %copy-start.1 = (s32[2,128]{1,0:T(2,128)S(1)}, s32[2,128]{1,0:T(2,128)}, u32[]{:S(2)}) copy-start(s32[2,128]{1,0:T(2,128)} %param.22) | copy-start | bytes 3076
  181.7 124.3 %copy-start.2 = (s32[2,128]{1,0:T(2,128)S(1)}, s32[2,128]{1,0:T(2,128)}, u32[]{:S(2)}) copy-start(s32[2,128]{1,0:T(2,128)} %param.23) | copy-start | bytes 3076
Sparse Core Ops, SparseCore 0:
  181.8 40.3 all-gather.2
